TPU v7x, 32 devices: a whole 2x2x4 slice. The times are simulated.
32 devices in a mesh: group: 1, seq: 16 (over z, y, x), batch: 1, head: 2 (over core).
Axes of the slice: x: 2, y: 2, z: 4, core: 2. Of those that a mesh axis runs over, the one named last changes fastest.
Arguments:
- queries: bfloat16 [2, 4, 128, 576], P(('group', 'batch'), None, ('seq', 'head')), may hold values from -40 to 40
- cache: bfloat16 [2, 32768, 576], P(('group', 'batch'), 'seq'), may hold values from -6 to 6
- lengths: int32 [2], P(('group', 'batch')), may hold values from 5 to 32768, as said below
Outputs:
- attended: bfloat16 [2, 4, 128, 512], P(('group', 'batch'), None, ('seq', 'head'))
Inputs may be any that keep to these rules, and one draw needn't show every extreme that they name: `lengths`: at least one sequence has length exactly 32768.
All inputs are finite; a program needn't handle non-finite values.
Results may differ from a plain program's by a relative error of at most 0.0065.
Values may be sent and summed in bfloat16 or wider, within the bound.
A program may use at most 64 MiB of HBM per device.

v0:
```python
import jax
import jax.numpy as jnp
from jax import lax
from jax.sharding import PartitionSpec as P

LAT = 512
ROPE = 64
NOPE = 128


def attend(query_rows, keys, lengths, positions):
    draft = query_rows.shape[1]
    scale = (NOPE + ROPE) ** (-0.5)
    scores = (
        jnp.einsum("bdhk,btk->bdht", query_rows, keys, preferred_element_type=jnp.float32) * scale
    )
    limit = lengths[:, None] - draft + jnp.arange(draft, dtype=jnp.int32)[None, :]
    visible = positions[None, None, None, :] <= limit[:, :, None, None]
    masked = jnp.where(visible, scores, jnp.float32(-1e30))
    peak = jnp.max(masked, axis=3)
    weights = jnp.where(visible, jnp.exp(masked - peak[..., None]), jnp.float32(0.0))
    total = jnp.sum(weights, axis=3)
    latent = keys[:, :, :LAT]
    numerator = jnp.einsum(
        "bdht,btl->bdhl", weights.astype(jnp.bfloat16), latent, preferred_element_type=jnp.float32
    )
    return (numerator, peak, total)


def body(queries, cache, lengths):
    tokens_here = cache.shape[1]
    seq_index = lax.axis_index("seq")
    query_rows = lax.all_gather(queries, "seq", axis=2, tiled=True)
    positions = seq_index * tokens_here + jnp.arange(tokens_here, dtype=jnp.int32)
    numerator, peak, total = attend(query_rows, cache, lengths, positions)
    highest = lax.pmax(peak, "seq")
    factor = jnp.exp(peak - highest)
    numerator, total = (
        lax.psum_scatter(numerator * factor[..., None], "seq", scatter_dimension=2, tiled=True),
        lax.psum_scatter(total * factor, "seq", scatter_dimension=2, tiled=True),
    )
    return (numerator / total[..., None]).astype(jnp.bfloat16)


def solution(mesh):
    return jax.shard_map(
        body,
        mesh=mesh,
        in_specs=(
            P(("group", "batch"), None, ("seq", "head"), None),
            P(("group", "batch"), "seq", None),
            P(("group", "batch")),
        ),
        out_specs=P(("group", "batch"), None, ("seq", "head"), None),
        check_vma=False,
    )
```

profile of v0, /device:TPU:0, one launch (start us, length us, event | category | flops | bytes accessed | tf_op | source)
XLA Modules:
  0.0 224.5 jit_solution(13620965935640238694)
XLA Ops:
  6.5 0.0 all-reduce.4.cloned.1.call-start
  6.5 0.7 broadcast_add_fusion
  7.2 0.1 iota_add_fusion.1
  7.3 0.8 copy.5
  8.1 46.3 %all_gather.3 = bf16[2,4,64,576]{3,1,0,2:T(4,128)(2,1)S(1)} all-gather(bf16[2,4,4,576]{3,1,0,2:T(4,128)(2,1)S(1)} %copy.5), channel_id=1, replica_groups=mesh['group'=1,'seq'=16,'batch'=1,'head'=2] {'seq'}, dimensions={2}, use_global_device_ids=true | all-gather | bytes 626688 | tf_op jit(solution)/shard_map/all_gather | solution.py:33
  54.4 0.1 broadcast_compare_fusion
  54.5 6.2 %fusion.5 = (f32[2,4,64]{2,1,0:T(4,128)S(1)}, f32[2,4,64,2048]{3,2,1,0:T(8,128)}) fusion(pred[2,4,2048]{2,1,0:T(4,128)(4,1)S(1)} %broadcast_compare_fusion, bf16[2,2048,576]{1,2,0:T(8,128)(2,1)} %param.4, bf16[2,4,64,576]{3,1,0,2:T(4,128)(2,1)S(1)} %all_gather.3), kind=kOutput, calls=%fused_computation.7 | convolution fusion | flops 1211104768 | bytes 9521152 | tf_op jit(solution)/shard_map/bdhk,btk->bdht/dot_general | solution.py:15
  60.6 36.5 %pmax.7 = f32[2,4,64]{2,1,0:T(4,128)S(1)} all-reduce(f32[2,4,64]{2,1,0:T(4,128)S(1)} %get-tuple-element.7), channel_id=1, replica_groups=mesh['group'=1,'seq'=16,'batch'=1,'head'=2] {'seq'}, use_global_device_ids=true, to_apply=%region_1.2 | all-reduce | flops 512 | bytes 4096 | tf_op jit(solution)/shard_map/pmax | solution.py:36
  97.2 0.0 copy-start
  97.2 3.7 %fusion.6 = f32[2,4,64]{2,1,0:T(4,128)S(1)} fusion(f32[2,4,64,2048]{3,2,1,0:T(8,128)} %get-tuple-element.8, f32[2,4,64]{2,1,0:T(4,128)S(1)} %get-tuple-element.7, pred[2,4,2048]{2,1,0:T(4,128)(4,1)S(1)} %broadcast_compare_fusion), kind=kLoop, calls=%fused_computation.8 | loop fusion | flops 5242368 | bytes 4214784 | tf_op jit(solution)/shard_map/reduce_sum | solution.py:22
  100.9 0.0 copy-done
  100.9 0.0 copy-start.1
  100.9 4.7 %fusion.14 = f32[2,4,64,512]{3,2,1,0:T(8,128)} fusion(bf16[2,2048,576]{1,2,0:T(8,128)(2,1)} %param.4, f32[2,4,64,2048]{3,2,1,0:T(8,128)S(1)} %copy-done, f32[2,4,64]{2,1,0:T(4,128)S(1)} %get-tuple-element.7, pred[2,4,2048]{2,1,0:T(4,128)(4,1)S(1)} %broadcast_compare_fusion, f32[2,4,64]{2,1,0:T(4,128)S(1)} %bitcast.29), kind=kOutput, calls=%fused_computation.15 | convolution fusion | flops 1079246848 | bytes 9457664 | tf_op jit(solution)/shard_map/bdht,btl->bdhl/dot_general | solution.py:24
  105.5 0.0 all-reduce.4.cloned.1.call-update
  105.6 0.0 copy-done.1
  105.6 0.6 dynamic-slice
  106.8 39.0 %all-reduce.1 = f32[2,4,64]{2,1,0:T(4,128)S(1)} all-reduce(f32[2,4,64]{2,1,0:T(4,128)S(1)} %bitcast.26), channel_id=3, replica_groups=mesh['group'=1,'seq'=16,'batch'=1,'head'=2] {'seq'}, use_global_device_ids=true, to_apply=%region_4.5.clone | all-reduce | flops 512 | bytes 4096
  145.8 0.1 constant_dynamic-slice_fusion
  145.8 70.2 %all-reduce.4.cloned.1.call-done = f32[2,4,64,512]{3,2,1,0:T(8,128)} async-done(((f32[2,4,64,512]{3,2,1,0:T(8,128)}), f32[2,4,64,512]{3,2,1,0:T(8,128)}) %all-reduce.4.cloned.1.call-update) | async-done | bytes 1048592
  216.0 1.6 fusion.20
  (2 shorter events, 0.0 us)
Async XLA Ops:
  6.5 209.5 %all-reduce.4.cloned.1.call-start = ((), (), s32[]{:S(2)}) async-start(), calls=%async_computation | async-start | bytes 2097152
  97.2 3.7 %copy-start = (f32[2,4,64,2048]{3,2,1,0:T(8,128)S(1)}, f32[2,4,64,2048]{3,2,1,0:T(8,128)}, u32[]{:S(2)}) copy-start(f32[2,4,64,2048]{3,2,1,0:T(8,128)} %get-tuple-element.8) | copy-start | bytes 12582916
  100.9 4.7 %copy-start.1 = (u32[32]{0:T(128)S(1)}, u32[32]{0:T(128)}, u32[]{:S(2)}) copy-start(u32[32]{0:T(128)} %constant.22) | copy-start | bytes 388
Sparse Core Ops, SparseCore 0:
  105.7 110.3 all-reduce.3
where the time goes:
time: 225 us; the launch traced here: 224 us
  blocking collectives  122 us (54%)
  waiting for transfers between devices  70.2 us (31%)
  between operations  14.1 us (6%)
  matrix products  10.8 us (5%)
  other arithmetic  6.09 us (3%)
    unnamed x2, waiting for transfers between devices  70.2 us
    all_gather x1, blocking collectives, body(): query_rows = lax.all_gather(queries, 'seq', axis=2, tiled=True)  46.3 us
    unnamed x1, blocking collectives  39 us
    pmax x1, blocking collectives, body(): highest = lax.pmax(peak, 'seq')  36.5 us
    dot_general x1, matrix products, attend(): jnp.einsum('bdhk,btk->bdht', query_rows, keys, preferred_element_type=jnp...  6.17 us
    dot_general x1, matrix products, attend(): jnp.einsum('bdht,btl->bdhl', weights.astype(jnp.bfloat16), latent, prefer...  4.66 us
  transfers between devices with their start and end apart: 1, of which 1 were waited for; matrix products, arithmetic and copies ran while one was open for 0% of the time, Pallas kernels for 0%

commit v1 on v0

v1 whole, which is shorter than its diff:
```python
import functools
import math

import jax
import jax.numpy as jnp
from jax import lax
from jax.experimental import pallas as pl
from jax.experimental.pallas import tpu as pltpu
from jax.sharding import PartitionSpec as P

LAT = 512
ROPE = 64
NOPE = 128
STAT = 128
MESH = pl.DeviceIdType.MESH
F32 = jnp.float32
BF16 = jnp.bfloat16


def kernel(
    planes,
    columns,
    len_ref,
    q_ref,
    cache_ref,
    out_ref,
    kv,
    gathered,
    scores,
    probs,
    part_out,
    part_in,
    line_out,
    line_in,
    kv_sem,
    z_send,
    z_recv,
    p_send,
    p_recv,
    a_send,
    a_recv,
    b_send,
    b_recv,
):
    batch, draft, heads, _ = q_ref.shape
    tokens = cache_ref.shape[2]
    rows = draft * heads
    total_rows = planes * columns * rows
    me = lax.axis_index("seq")
    z = me // planes
    p = me % planes
    scale = (NOPE + ROPE) ** (-0.5) * math.log2(math.e)

    def to_plane(j):
        if planes == 4:
            return (p + 1 - 2 * (p % 2), (p + 2) % 4, 3 - p)[j - 1]
        return (p + j) % planes

    def to_line(k):
        return (z + k) % columns

    def from_line(k):
        return (z + columns - k) % columns

    def remote(src, dst, send, recv, seq):
        return pltpu.make_async_remote_copy(
            src_ref=src,
            dst_ref=dst,
            send_sem=send,
            recv_sem=recv,
            device_id={"seq": seq},
            device_id_type=MESH,
        )

    loads = [
        pltpu.make_async_copy(cache_ref.at[b], kv.at[b], kv_sem.at[b]) for b in range(batch)
    ]
    for load in loads:
        load.start()

    barrier = pltpu.get_barrier_semaphore()
    peers = [z * planes + to_plane(j) for j in range(1, planes)]
    peers += [to_line(k) * planes + p for k in range(1, columns)]
    for peer in peers:
        pl.semaphore_signal(barrier, inc=1, device_id={"seq": peer}, device_id_type=MESH)

    for b in range(batch):
        for d in range(draft):
            gathered[b, p, z, d * heads : (d + 1) * heads, :] = q_ref[b, d]
    pl.semaphore_wait(barrier, len(peers))

    def line_copy(b, k):
        block = gathered.at[b, p, z]
        return remote(block, block, z_send.at[b, k], z_recv.at[b, k], to_line(k) * planes + p)

    def plane_copy(b, k, j):
        block = gathered.at[b, p, from_line(k)]
        return remote(
            block, block, p_send.at[b, k, j], p_recv.at[b, k, j], z * planes + to_plane(j)
        )

    sent = []
    for b in range(batch):
        for k in range(1, columns):
            copy = line_copy(b, k)
            copy.start()
            sent.append(copy)
    for b in range(batch):
        for k in range(columns):
            if k:
                line_copy(b, k).wait_recv()
            for j in range(planes - 1, 0, -1):
                copy = plane_copy(b, k, j)
                copy.start()
                sent.append(copy)

    tile = min(512, tokens)
    row = lax.broadcasted_iota(jnp.int32, (total_rows, 1), 0)
    step = (row % rows) // heads - draft - me * tokens
    lane = lax.broadcasted_iota(jnp.int32, (total_rows, tile), 1)
    stat_lane = lax.broadcasted_iota(jnp.int32, (total_rows, STAT), 1)

    def attend(b):
        q = gathered[b].reshape(total_rows, q_ref.shape[3])
        limit = step + len_ref[b]
        peak = jnp.full((total_rows, 1), -1e20, F32)
        for t in range(0, tokens, tile):
            s = lax.dot_general(
                q, kv[b, :, t : t + tile], (((1,), (0,)), ((), ())), preferred_element_type=F32
            )
            s = jnp.where(lane <= limit - t, s * scale, -1e30)
            scores[:, t : t + tile] = s
            peak = jnp.maximum(peak, jnp.max(s, axis=1, keepdims=True))
        peak = peak.astype(BF16).astype(F32)
        total = jnp.zeros((total_rows, 1), F32)
        for t in range(0, tokens, tile):
            w = jnp.exp2(scores[:, t : t + tile] - peak)
            total = total + jnp.sum(w, axis=1, keepdims=True)
            probs[:, t : t + tile] = w.astype(BF16)
        numerator = lax.dot_general(
            probs[...], kv[b, :LAT, :], (((1,), (1,)), ((), ())), preferred_element_type=F32
        )
        part_out[b, :, :, :, :LAT] = numerator.astype(BF16).reshape(planes, columns, rows, LAT)
        part_out[b, :, :, :, LAT:] = pack(stat_lane, peak, total).reshape(
            planes, columns, rows, STAT
        )

    def pack(lanes, peak, total):
        high = total.astype(BF16).astype(F32)
        stats = jnp.where(lanes == 0, peak, jnp.where(lanes == 1, high, total - high))
        return stats.astype(BF16)

    def merge(parts):
        stats = [x[:, LAT:].astype(F32) for x in parts]
        peaks = [x[:, 0:1] for x in stats]
        peak = functools.reduce(jnp.maximum, peaks)
        factors = [jnp.exp2(x - peak) for x in peaks]
        total = sum(f * (x[:, 1:2] + x[:, 2:3]) for f, x in zip(factors, stats))
        numerator = sum(f * x[:, :LAT].astype(F32) for f, x in zip(factors, parts))
        return numerator, peak, total

    def plane_part(b, j):
        other = to_plane(j)
        return remote(
            part_out.at[b, other],
            part_in.at[b, j],
            a_send.at[b, j],
            a_recv.at[b, j],
            z * planes + other,
        )

    def line_part(b, k):
        other = to_line(k)
        return remote(
            line_out.at[b, other],
            line_in.at[b, k],
            b_send.at[b, k],
            b_recv.at[b, k],
            other * planes + p,
        )

    for b in range(batch):
        for k in range(columns):
            for j in range(planes - 1, 0, -1):
                plane_copy(b, k, j).wait_recv()
        loads[b].wait()
        attend(b)
        for j in range(planes - 1, 0, -1):
            copy = plane_part(b, j)
            copy.start()
            sent.append(copy)

    line_rows = columns * rows
    for b in range(batch):
        parts = [part_out[b, p].reshape(line_rows, LAT + STAT)]
        for j in range(1, planes):
            plane_part(b, j).wait_recv()
            parts.append(part_in[b, j].reshape(line_rows, LAT + STAT))
        numerator, peak, total = merge(parts)
        line_out[b, :, :, :LAT] = numerator.astype(BF16).reshape(columns, rows, LAT)
        line_out[b, :, :, LAT:] = pack(stat_lane[:line_rows], peak, total).reshape(
            columns, rows, STAT
        )
        for k in range(columns - 1, 0, -1):
            copy = line_part(b, k)
            copy.start()
            sent.append(copy)

    for b in range(batch):
        parts = [line_out[b, z]]
        for k in range(1, columns):
            line_part(b, k).wait_recv()
            parts.append(line_in[b, k])
        numerator, peak, total = merge(parts)
        result = (numerator / total).astype(BF16)
        for d in range(draft):
            out_ref[b, d] = result[d * heads : (d + 1) * heads]

    for copy in sent:
        copy.wait_send()


def body(ways, queries, cache, lengths):
    batch, draft, heads, depth = queries.shape
    tokens = cache.shape[1]
    rows = draft * heads
    planes = max(i for i in range(1, ways + 1) if ways % i == 0 and i * i <= ways)
    columns = ways // planes
    vmem = pl.BlockSpec(memory_space=pltpu.VMEM)
    dma = pltpu.SemaphoreType.DMA
    width = LAT + STAT
    return pl.pallas_call(
        functools.partial(kernel, planes, columns),
        out_shape=jax.ShapeDtypeStruct((batch, draft, heads, LAT), BF16),
        in_specs=[
            pl.BlockSpec(memory_space=pltpu.SMEM),
            vmem,
            pl.BlockSpec(memory_space=pltpu.HBM),
        ],
        out_specs=vmem,
        scratch_shapes=[
            pltpu.VMEM((batch, depth, tokens), BF16),
            pltpu.VMEM((batch, planes, columns, rows, depth), BF16),
            pltpu.VMEM((ways * rows, tokens), F32),
            pltpu.VMEM((ways * rows, tokens), BF16),
            pltpu.VMEM((batch, planes, columns, rows, width), BF16),
            pltpu.VMEM((batch, planes, columns, rows, width), BF16),
            pltpu.VMEM((batch, columns, rows, width), BF16),
            pltpu.VMEM((batch, columns, rows, width), BF16),
            dma((batch,)),
            dma((batch, columns)),
            dma((batch, columns)),
            dma((batch, columns, planes)),
            dma((batch, columns, planes)),
            dma((batch, planes)),
            dma((batch, planes)),
            dma((batch, columns)),
            dma((batch, columns)),
        ],
        compiler_params=pltpu.CompilerParams(
            collective_id=0,
            has_side_effects=True,
            vmem_limit_bytes=48 * 1024 * 1024,
        ),
    )(lengths, queries, jnp.swapaxes(cache, 1, 2))


def solution(mesh):
    return jax.shard_map(
        functools.partial(body, mesh.shape["seq"]),
        mesh=mesh,
        in_specs=(
            P(("group", "batch"), None, ("seq", "head"), None),
            P(("group", "batch"), "seq", None),
            P(("group", "batch")),
        ),
        out_specs=P(("group", "batch"), None, ("seq", "head"), None),
        check_vma=False,
    )
```

time: 225 us -> 34.8 us (0.15)
  blocking collectives: 122 us -> 0 us
  waiting for transfers between devices: 70.2 us -> 0 us
  Pallas kernels: 0 us -> 30.1 us
  between operations: 14.1 us -> 0.01 us
  matrix products: 10.8 us -> 0 us
  other arithmetic: 6.09 us -> 0 us
  local copies, waits for them, and re-layouts: 1.46 us -> 4.39 us
    unnamed x2 -> x0, waiting for transfers between devices: 70.2 us -> none
    all_gather x1 -> x0, blocking collectives: 46.3 us -> none  [body(): query_rows = lax.all_gather(queries, 'seq', axis=2, tiled=True)]
    unnamed x1 -> x0, blocking collectives: 39 us -> none
    pmax x1 -> x0, blocking collectives: 36.5 us -> none  [body(): highest = lax.pmax(peak, 'seq')]
    pallas_call x0 -> x1, Pallas kernels: none -> 30.1 us  [body(): pl.pallas_call(functools.partial(kernel, planes, columns), out_shape=jax....]
    dot_general x2 -> x0, matrix products: 10.8 us -> none  [the longest x1 6.17 us: attend(): jnp.einsum('bdhk,btk->bdht', query_rows, keys, preferred_element_type=jnp...]
    reduce_sum x1 -> x0, other arithmetic: 3.65 us -> none  [attend(): total = jnp.sum(weights, axis=3)]
    unnamed x7, local copies, waits for them, and re-layouts: 1.46 us -> 4.39 us
  transfers between devices with their start and end apart: 1 -> 0, of which waited for: 1 -> 0; matrix products, arithmetic and copies ran while one was open for 0% -> 0% of each run, Pallas kernels for 0% -> 0%
where the time goes in v1:
time: 34.8 us; the launch traced here: 34.5 us
  Pallas kernels  30.1 us (86%)
  local copies, waits for them, and re-layouts  4.39 us (13%)
    pallas_call x1, Pallas kernels, body(): pl.pallas_call(functools.partial(kernel, planes, columns), out_shape=jax....  30.1 us
    unnamed x7, local copies, waits for them, and re-layouts  4.39 us

profile of v1, /device:TPU:0, one launch (start us, length us, event | category | flops | bytes accessed | tf_op | source)
XLA Modules:
  0.0 34.5 jit_solution(14428665148022776358)
XLA Ops:
  0.0 0.0 copy-start
  0.0 2.3 %copy-done = bf16[2,2048,576]{1,2,0:T(8,128)(2,1)S(1)} copy-done((bf16[2,2048,576]{1,2,0:T(8,128)(2,1)S(1)}, bf16[2,2048,576]{1,2,0:T(8,128)(2,1)}, u32[]{:S(2)}) %copy-start) | copy-done | bytes 4718616
  2.3 0.0 copy-start.1
  2.3 0.8 %copy-done.1 = bf16[2,4,4,576]{3,2,1,0:T(4,128)(2,1)S(1)} copy-done((bf16[2,4,4,576]{3,2,1,0:T(4,128)(2,1)S(1)}, bf16[2,4,4,576]{3,2,1,0:T(4,128)(2,1)}, u32[]{:S(2)}) %copy-start.1) | copy-done | bytes 36888
  3.1 0.0 copy-start.2
  3.1 0.7 %copy-done.2 = s32[2]{0:T(128)S(1)} copy-done((s32[2]{0:T(128)S(1)}, s32[2]{0:T(128)}, u32[]{:S(2)}) %copy-start.2) | copy-done | bytes 32
  3.8 30.1 %shard_map.37 = bf16[2,4,4,512]{3,2,1,0:T(4,128)(2,1)S(1)} custom-call(s32[2]{0:T(128)S(1)} %copy-done.2, bf16[2,4,4,576]{3,2,1,0:T(4,128)(2,1)S(1)} %copy-done.1, bf16[2,576,2048]{2,1,0:T(8,128)(2,1)S(1)} %bitcast.1), custom_call_target="tpu_custom_call" | custom-call | tf_op jit(solution)/shard_map/pallas_call | solution.py:232
  33.9 0.6 %copy.5 = bf16[2,4,4,512]{3,2,1,0:T(4,128)(2,1)} copy(bf16[2,4,4,512]{3,2,1,0:T(4,128)(2,1)S(1)} %shard_map.37) | data formatting | bytes 65536
Async XLA Ops:
  0.0 2.3 %copy-start = (bf16[2,2048,576]{1,2,0:T(8,128)(2,1)S(1)}, bf16[2,2048,576]{1,2,0:T(8,128)(2,1)}, u32[]{:S(2)}) copy-start(bf16[2,2048,576]{1,2,0:T(8,128)(2,1)} %param.4) | copy-start | bytes 14155780
  2.3 0.8 %copy-start.1 = (bf16[2,4,4,576]{3,2,1,0:T(4,128)(2,1)S(1)}, bf16[2,4,4,576]{3,2,1,0:T(4,128)(2,1)}, u32[]{:S(2)}) copy-start(bf16[2,4,4,576]{3,2,1,0:T(4,128)(2,1)} %q_ref.1) | copy-start | bytes 110596
  3.1 0.7 %copy-start.2 = (s32[2]{0:T(128)S(1)}, s32[2]{0:T(128)}, u32[]{:S(2)}) copy-start(s32[2]{0:T(128)} %len_ref.1) | copy-start | bytes 28

commit v2 on v1

v2 whole, which is shorter than its diff:
```python
import functools
import math

import jax
import jax.numpy as jnp
from jax import lax
from jax.experimental import pallas as pl
from jax.experimental.pallas import tpu as pltpu
from jax.sharding import PartitionSpec as P

LAT = 512
ROPE = 64
NOPE = 128
STAT = 128
MESH = pl.DeviceIdType.MESH
F32 = jnp.float32
BF16 = jnp.bfloat16


def kernel(
    planes,
    columns,
    len_hbm,
    q_hbm,
    cache_ref,
    out_ref,
    len_ref,
    q_ref,
    kv,
    gathered,
    scores,
    probs,
    part_out,
    part_in,
    stat_out,
    stat_in,
    line_out,
    line_in,
    in_sem,
    kv_sem,
    z_send,
    z_recv,
    p_send,
    p_recv,
    a_send,
    a_recv,
    s_send,
    s_recv,
    b_send,
    b_recv,
):
    batch, draft, heads, _ = q_ref.shape
    tokens = cache_ref.shape[2]
    rows = draft * heads
    total_rows = planes * columns * rows
    me = lax.axis_index("seq")
    z = me // planes
    p = me % planes
    scale = (NOPE + ROPE) ** (-0.5) * math.log2(math.e)

    def to_plane(j):
        if planes == 4:
            return (p + 1 - 2 * (p % 2), (p + 2) % 4, 3 - p)[j - 1]
        return (p + j) % planes

    half = z // (columns - columns // 2)
    far = (1 - half) * (columns - 1)
    gap = far + (2 * half - 1) * z

    def line(i):
        return far + (2 * half - 1) * (i + (i + columns - gap) // columns)

    def remote(src, dst, send, recv, seq):
        return pltpu.make_async_remote_copy(
            src_ref=src,
            dst_ref=dst,
            send_sem=send,
            recv_sem=recv,
            device_id={"seq": seq},
            device_id_type=MESH,
        )

    loads = [
        pltpu.make_async_copy(cache_ref.at[b], kv.at[b], kv_sem.at[b]) for b in range(batch)
    ]
    small = [
        pltpu.make_async_copy(q_hbm, q_ref, in_sem.at[0]),
        pltpu.make_async_copy(len_hbm, len_ref, in_sem.at[1]),
    ]
    for load in small:
        load.start()

    barrier = pltpu.get_barrier_semaphore()
    peers = [z * planes + to_plane(j) for j in range(1, planes)]
    peers += [line(i) * planes + p for i in range(columns - 1)]
    for peer in peers:
        pl.semaphore_signal(barrier, inc=1, device_id={"seq": peer}, device_id_type=MESH)

    for load in loads:
        load.start()
    for load in small:
        load.wait()
    for b in range(batch):
        for d in range(draft):
            gathered[b, p, z, d * heads : (d + 1) * heads, :] = q_ref[b, d]
    pl.semaphore_wait(barrier, len(peers))

    def line_copy(b, i):
        block = gathered.at[b, p, z]
        return remote(block, block, z_send.at[b, i], z_recv.at[b, z], line(i) * planes + p)

    def line_arrival(b, i):
        other = line(i)
        block = gathered.at[b, p, other]
        return remote(block, block, z_send.at[b, i], z_recv.at[b, other], other * planes + p)

    def plane_copy(b, source, j):
        block = gathered.at[b, p, source]
        return remote(
            block,
            block,
            p_send.at[b, source, j],
            p_recv.at[b, source, j],
            z * planes + to_plane(j),
        )

    sent = []

    def start(copy):
        copy.start()
        sent.append(copy)

    for b in range(batch):
        for i in range(columns - 1):
            start(line_copy(b, i))
    for b in range(batch):
        for j in range(planes - 1, 0, -1):
            start(plane_copy(b, z, j))
    for b in range(batch):
        for i in range(columns - 2, -1, -1):
            line_arrival(b, i).wait_recv()
            for j in range(planes - 1, 0, -1):
                start(plane_copy(b, line(i), j))

    tile = min(512, tokens)
    row = lax.broadcasted_iota(jnp.int32, (total_rows, 1), 0)
    step = (row % rows) // heads - draft - me * tokens
    lane = lax.broadcasted_iota(jnp.int32, (total_rows, tile), 1)
    stat_lane = lax.broadcasted_iota(jnp.int32, (planes, rows, STAT), 2)

    def attend(b):
        q = gathered[b].reshape(total_rows, q_ref.shape[3])
        limit = step + len_ref[b]
        peak = jnp.full((total_rows, 1), -1e20, F32)
        for t in range(0, tokens, tile):
            s = lax.dot_general(
                q, kv[b, :, t : t + tile], (((1,), (0,)), ((), ())), preferred_element_type=F32
            )
            s = jnp.where(lane <= limit - t, s * scale, -1e30)
            scores[:, t : t + tile] = s
            peak = jnp.maximum(peak, jnp.max(s, axis=1, keepdims=True))
        peak = peak.astype(BF16).astype(F32)
        total = jnp.zeros((total_rows, 1), F32)
        for t in range(0, tokens, tile):
            w = jnp.exp2(scores[:, t : t + tile] - peak)
            total = total + jnp.sum(w, axis=1, keepdims=True)
            probs[:, t : t + tile] = w.astype(BF16)
        numerator = lax.dot_general(
            probs[...], kv[b, :LAT, :], (((1,), (1,)), ((), ())), preferred_element_type=F32
        )
        part_out[b] = numerator.astype(BF16).reshape(planes, columns, rows, LAT)
        high = total.astype(BF16).astype(F32)
        stats = jnp.zeros((planes, rows, STAT), F32)
        for n, x in enumerate((peak, high, total - high)):
            x = x.reshape(planes, columns, rows, 1)
            for c in range(columns):
                stats = jnp.where(stat_lane == 3 * c + n, x[:, c], stats)
        stat_out[b] = stats.astype(BF16)

    def merge(stats, parts):
        peak = functools.reduce(jnp.maximum, [x[0] for x in stats])
        factors = [jnp.exp2(x[0] - peak) for x in stats]
        total = sum(f * (x[1] + x[2]) for f, x in zip(factors, stats))
        numerator = sum(f * x.astype(F32) for f, x in zip(factors, parts))
        return numerator, peak, total

    small_lane = lax.broadcasted_iota(jnp.int32, (rows, STAT), 1)

    def plane_stats(x, c):
        x = x.astype(F32)
        return [
            jnp.sum(jnp.where(small_lane == 3 * c + n, x, 0.0), axis=1, keepdims=True)
            for n in range(3)
        ]

    def line_stats(tile):
        x = tile[:, LAT:].astype(F32)
        return [x[:, n : n + 1] for n in range(3)]

    def plane_part(b, c, j):
        other = to_plane(j)
        return remote(
            part_out.at[b, other, c],
            part_in.at[b, j, c],
            a_send.at[b, c, j],
            a_recv.at[b, c, j],
            z * planes + other,
        )

    def plane_stat(b, j):
        other = to_plane(j)
        return remote(
            stat_out.at[b, other],
            stat_in.at[b, j],
            s_send.at[b, j],
            s_recv.at[b, j],
            z * planes + other,
        )

    def line_part(b, i):
        other = line(i)
        return remote(
            line_out.at[b, other],
            line_in.at[b, z],
            b_send.at[b, i],
            b_recv.at[b, z],
            other * planes + p,
        )

    def line_part_arrival(b, i):
        other = line(i)
        return remote(
            line_out.at[b, other],
            line_in.at[b, other],
            b_send.at[b, i],
            b_recv.at[b, other],
            other * planes + p,
        )

    def plane_merge(b, c):
        parts = [part_out[b, p, c]]
        stats = [plane_stats(stat_out[b, p], c)]
        for j in range(1, planes):
            plane_part(b, c, j).wait_recv()
            parts.append(part_in[b, j, c])
            stats.append(plane_stats(stat_in[b, j], c))
        return merge(stats, parts)

    order = [line(i) for i in range(columns - 1)] + [z]
    for b in range(batch):
        for c in range(columns):
            for j in range(planes - 1, 0, -1):
                plane_copy(b, c, j).wait_recv()
        loads[b].wait()
        attend(b)
        for j in range(planes - 1, 0, -1):
            start(plane_stat(b, j))
        for c in order:
            for j in range(planes - 1, 0, -1):
                start(plane_part(b, c, j))

    own = []
    for b in range(batch):
        for j in range(1, planes):
            plane_stat(b, j).wait_recv()
        for i in range(columns - 1):
            numerator, peak, total = plane_merge(b, line(i))
            high = total.astype(BF16).astype(F32)
            packed = jnp.where(
                small_lane == 0, peak, jnp.where(small_lane == 1, high, total - high)
            )
            line_out[b, line(i), :, :LAT] = numerator.astype(BF16)
            line_out[b, line(i), :, LAT:] = packed.astype(BF16)
            start(line_part(b, i))
        own.append(plane_merge(b, z))

    for b in range(batch):
        numerator, peak, total = own[b]
        stats, parts = [[peak, total, 0.0]], [numerator]
        for i in range(columns - 2, -1, -1):
            line_part_arrival(b, i).wait_recv()
            block = line_in[b, line(i)]
            stats.append(line_stats(block))
            parts.append(block[:, :LAT])
        numerator, _, total = merge(stats, parts)
        result = (numerator / total).astype(BF16)
        for d in range(draft):
            out_ref[b, d] = result[d * heads : (d + 1) * heads]

    for copy in sent:
        copy.wait_send()


def body(ways, queries, cache, lengths):
    batch, draft, heads, depth = queries.shape
    tokens = cache.shape[1]
    rows = draft * heads
    planes = max(i for i in range(1, ways + 1) if ways % i == 0 and i * i <= ways)
    columns = ways // planes
    dma = pltpu.SemaphoreType.DMA
    width = LAT + STAT
    return pl.pallas_call(
        functools.partial(kernel, planes, columns),
        out_shape=jax.ShapeDtypeStruct((batch, draft, heads, LAT), BF16),
        in_specs=[
            pl.BlockSpec(memory_space=pl.ANY),
            pl.BlockSpec(memory_space=pl.ANY),
            pl.BlockSpec(memory_space=pl.ANY),
        ],
        out_specs=pl.BlockSpec(memory_space=pltpu.VMEM),
        scratch_shapes=[
            pltpu.SMEM(lengths.shape, jnp.int32),
            pltpu.VMEM(queries.shape, BF16),
            pltpu.VMEM((batch, depth, tokens), BF16),
            pltpu.VMEM((batch, planes, columns, rows, depth), BF16),
            pltpu.VMEM((ways * rows, tokens), F32),
            pltpu.VMEM((ways * rows, tokens), BF16),
            pltpu.VMEM((batch, planes, columns, rows, LAT), BF16),
            pltpu.VMEM((batch, planes, columns, rows, LAT), BF16),
            pltpu.VMEM((batch, planes, rows, STAT), BF16),
            pltpu.VMEM((batch, planes, rows, STAT), BF16),
            pltpu.VMEM((batch, columns, rows, width), BF16),
            pltpu.VMEM((batch, columns, rows, width), BF16),
            dma((2,)),
            dma((batch,)),
            dma((batch, columns)),
            dma((batch, columns)),
            dma((batch, columns, planes)),
            dma((batch, columns, planes)),
            dma((batch, columns, planes)),
            dma((batch, columns, planes)),
            dma((batch, planes)),
            dma((batch, planes)),
            dma((batch, columns)),
            dma((batch, columns)),
        ],
        compiler_params=pltpu.CompilerParams(
            collective_id=0,
            has_side_effects=True,
            vmem_limit_bytes=50331648,
        ),
    )(pltpu.with_memory_space_constraint(lengths, pltpu.HBM), pltpu.with_memory_space_constraint(queries, pltpu.HBM), pltpu.with_memory_space_constraint(jnp.swapaxes(cache, 1, 2), pltpu.HBM))


def solution(mesh):
    return jax.shard_map(
        functools.partial(body, mesh.shape["seq"]),
        mesh=mesh,
        in_specs=(
            P(("group", "batch"), None, ("seq", "head"), None),
            P(("group", "batch"), "seq", None),
            P(("group", "batch")),
        ),
        out_specs=P(("group", "batch"), None, ("seq", "head"), None),
        check_vma=False,
    )
```

time: 34.8 us -> 27.5 us (0.79)
  local copies, waits for them, and re-layouts: 4.39 us -> 0.62 us
  Pallas kernels: 30.1 us -> 26.8 us
    unnamed x7 -> x1, local copies, waits for them, and re-layouts: 4.39 us -> 0.62 us
    pallas_call x1, Pallas kernels: 30.1 us -> 26.8 us  [body(): pl.pallas_call(functools.partial(kernel, planes, columns), out_shape=jax....]
where the time goes in v2:
time: 27.5 us; the launch traced here: 27.4 us
  Pallas kernels  26.8 us (97%)
  local copies, waits for them, and re-layouts  0.62 us (2%)
    pallas_call x1, Pallas kernels, body(): pl.pallas_call(functools.partial(kernel, planes, columns), out_shape=jax....  26.8 us
    unnamed x1, local copies, waits for them, and re-layouts  0.62 us

profile of v2, /device:TPU:0, one launch (start us, length us, event | category | flops | bytes accessed | tf_op | source)
XLA Modules:
  0.0 27.4 jit_solution(2087733841370037818)
XLA Ops:
  0.0 26.8 %shard_map.37 = bf16[2,4,4,512]{3,2,1,0:T(4,128)(2,1)S(1)} custom-call(s32[2]{0:T(128)} %len_hbm.1, bf16[2,4,4,576]{3,2,1,0:T(4,128)(2,1)} %q_hbm.1, bf16[2,576,2048]{2,1,0:T(8,128)(2,1)} %bitcast.1), custom_call_target="tpu_custom_call" | custom-call | tf_op jit(solution)/shard_map/pallas_call | solution.py:302
  26.8 0.6 %copy.5 = bf16[2,4,4,512]{3,2,1,0:T(4,128)(2,1)} copy(bf16[2,4,4,512]{3,2,1,0:T(4,128)(2,1)S(1)} %shard_map.37) | data formatting | bytes 65536

commit v3 on v2

--- a/solution.py
+++ b/solution.py
@@ -142,7 +142,7 @@
             for j in range(planes - 1, 0, -1):
                 start(plane_copy(b, line(i), j))
 
-    tile = min(512, tokens)
+    tile = min(256, tokens)
     row = lax.broadcasted_iota(jnp.int32, (total_rows, 1), 0)
     step = (row % rows) // heads - draft - me * tokens
     lane = lax.broadcasted_iota(jnp.int32, (total_rows, tile), 1)

time: 27.5 us -> 27.5 us (level)
  no operation moved by 1% of the time
where the time goes in v3:
time: 27.5 us; the launch traced here: 27.3 us
  Pallas kernels  26.7 us (97%)
  local copies, waits for them, and re-layouts  0.62 us (2%)
    pallas_call x1, Pallas kernels, body(): pl.pallas_call(functools.partial(kernel, planes, columns), out_shape=jax....  26.7 us
    unnamed x1, local copies, waits for them, and re-layouts  0.62 us

profile of v3, /device:TPU:0, one launch (start us, length us, event | category | flops | bytes accessed | tf_op | source)
XLA Modules:
  0.0 27.3 jit_solution(7652150627584564433)
XLA Ops:
  0.0 26.7 %shard_map.37 = bf16[2,4,4,512]{3,2,1,0:T(4,128)(2,1)S(1)} custom-call(s32[2]{0:T(128)} %len_hbm.1, bf16[2,4,4,576]{3,2,1,0:T(4,128)(2,1)} %q_hbm.1, bf16[2,576,2048]{2,1,0:T(8,128)(2,1)} %bitcast.1), custom_call_target="tpu_custom_call" | custom-call | tf_op jit(solution)/shard_map/pallas_call | solution.py:302
  26.7 0.6 %copy.5 = bf16[2,4,4,512]{3,2,1,0:T(4,128)(2,1)} copy(bf16[2,4,4,512]{3,2,1,0:T(4,128)(2,1)S(1)} %shard_map.37) | data formatting | bytes 65536
